TPU v7x, 32 devices: a whole 2x2x4 slice. The times are simulated.
32 devices in a mesh: band: 8 (over y, x, core), ga: 4 (over z).
Axes of the slice: x: 2, y: 2, z: 4, core: 2. Of those that a mesh axis runs over, the one named last changes fastest.
Arguments:
- orbitals: bfloat16 [256, 90112], P(('band', 'ga')), may hold values from -6 to 6
- local_part: bfloat16 [256, 90112], P(('band', 'ga')), may hold values from -6 to 6
- projectors: bfloat16 [90112, 1664], P(('band', 'ga')), may hold values from -0.01953125 to 0.01953125
- couplings: float32 [4, 13, 13], replicated, may hold values from -20 to 20, as said below
- species: int32 [128], replicated, may hold values from 0 to 3
Outputs:
- applied: bfloat16 [256, 90112], P(('band', 'ga'))
Inputs may be any that keep to these rules, and one draw needn't show every extreme that they name: `couplings`: each species has one symmetric block.
All inputs are finite; a program needn't handle non-finite values.
Results may differ from a plain program's by a relative error of at most 0.0056.
Values may be sent and summed in bfloat16 or wider, within the bound.
A program may use at most 64 MiB of HBM per device.

v0:
```python
import jax
import jax.numpy as jnp
from jax import lax
from jax.sharding import PartitionSpec as P


def select_blocks(couplings, species):
    kinds = couplings.shape[0]
    width = couplings.shape[1]
    select = (jnp.arange(kinds, dtype=jnp.int32)[:, None] == species[None, :]).astype(jnp.float32)
    table = jnp.einsum(
        "sk,sa->ka",
        couplings.reshape(kinds, width * width),
        select,
        precision=lax.Precision.HIGHEST,
    )
    return table.reshape(width, width, species.shape[0])


def couple(totals, blocks):
    width = blocks.shape[0]
    atom_count = blocks.shape[2]
    folded = totals.reshape(totals.shape[0], width, atom_count)
    mixed = jnp.zeros_like(folded)
    for inner in range(width):
        mixed = mixed + folded[:, inner, None, :] * blocks[None, inner, :, :]
    return mixed.reshape(totals.shape[0], width * atom_count).astype(jnp.bfloat16)


def expand(coefs, projectors):
    return jnp.einsum("bp,gp->bg", coefs, projectors, preferred_element_type=jnp.float32).astype(
        jnp.bfloat16
    )


def on_device(orbitals, local_part, projectors, couplings, species):
    blocks = select_blocks(couplings, species)
    slab_orbitals = lax.all_to_all(
        orbitals, ("band", "ga"), split_axis=1, concat_axis=0, tiled=True
    )
    partial_value = jnp.dot(slab_orbitals, projectors, preferred_element_type=jnp.float32)
    totals = lax.psum(partial_value, ("band", "ga"))
    slab_correction = expand(couple(totals, blocks), projectors)
    correction = lax.all_to_all(
        slab_correction, ("band", "ga"), split_axis=0, concat_axis=1, tiled=True
    )
    correction = lax.optimization_barrier(correction)
    return (local_part.astype(jnp.float32) + correction.astype(jnp.float32)).astype(jnp.bfloat16)


def solution(mesh):
    placed = (P(("band", "ga"), None), P(("band", "ga"), None), P(("band", "ga"), None), P(), P())
    return jax.shard_map(
        on_device, mesh=mesh, in_specs=placed, out_specs=P(("band", "ga"), None), check_vma=False
    )
```

profile of v0, /device:TPU:1, one launch (start us, length us, event | category | flops | bytes accessed | tf_op | source)
XLA Modules:
  0.0 247.2 jit_solution(7646724141969409436)
XLA Ops:
  6.5 0.0 all-reduce.2.cloned.1.call-start
  6.5 42.4 %all_to_all.38 = bf16[8,32,2816]{2,0,1:T(8,128)(2,1)S(1)} all-to-all(bf16[8,32,2816]{2,0,1:T(8,128)(2,1)} %bitcast.148), channel_id=1, replica_groups=mesh['band'=8,'ga'=4] {'band','ga'}, dimensions={1} | all-to-all | bytes 2883584 | tf_op jit(solution)/shard_map/all_to_all | solution.py:38
  48.9 8.6 %fusion.14 = f32[256,1664]{0,1:T(8,128)} fusion(bf16[2816,1664]{1,0:T(8,128)(2,1)} %param.7, bf16[8,32,2816]{2,0,1:T(8,128)(2,1)S(1)} %all_to_all.38), kind=kOutput, calls=%fused_computation.29 | convolution fusion | flops 2399141888 | bytes 12517376 | tf_op jit(solution)/shard_map/dot_general | solution.py:41
  57.5 0.0 copy-start.1
  57.5 0.0 copy-start.2
  57.5 0.0 all-reduce.2.cloned.1.call-update
  57.6 0.7 copy-done.1
  58.3 0.1 reshape.81
  58.4 0.0 copy-done.2
  58.4 0.3 convolution_bitcast_fusion
  58.7 129.1 %all-reduce.2.cloned.1.call-done = f32[256,13,128]{0,2,1:T(8,128)} async-done(((f32[256,13,128]{0,2,1:T(8,128)}), f32[256,13,128]{0,2,1:T(8,128)}) %all-reduce.2.cloned.1.call-update) | async-done | bytes 1703952 | tf_op jit(solution)/shard_map/psum | solution.py:42
  187.8 1.6 slice_bitcast_fusion.12
  189.3 3.0 %fusion.2 = bf16[256,1664]{0,1:T(8,128)(2,1)S(1)} fusion(f32[1664]{0:T(1024)S(1)} %get-tuple-element.19, f32[256,128]{0,1:T(8,128)S(1)} %get-tuple-element.6, f32[1664]{0:T(1024)S(1)} %get-tuple-element.20, f32[256,128]{0,1:T(8,128)S(1)} %get-tuple-element.7, f32[1664]{0:T(1024)S(1)} %get-tuple-element.21, f32[256,128]{0,1:T(8,128)S(1)} %get-tuple-element.8, ...), kind=kLoop, calls=%fused_computation.5 | loop fusion | flops 11075584 | bytes 2642432 | tf_op jit(solution)/shard_map/convert_element_type | solution.py:27
  192.3 6.6 %fusion = bf16[32,8,2816]{2,1,0:T(8,128)(2,1)S(1)} fusion(bf16[256,1664]{0,1:T(8,128)(2,1)S(1)} %fusion.2, bf16[2816,1664]{1,0:T(8,128)(2,1)} %param.7), kind=kOutput, calls=%fused_computation.1 | convolution fusion | flops 2399862784 | bytes 11665408 | tf_op jit(solution)/shard_map/bp,gp->bg/dot_general | solution.py:31
  198.9 0.0 copy-start
  198.9 40.0 %all_to_all.39 = bf16[32,8,2816]{2,1,0:T(8,128)(2,1)S(1)} all-to-all(bf16[32,8,2816]{2,1,0:T(8,128)(2,1)S(1)} %fusion), channel_id=1, replica_groups=mesh['band'=8,'ga'=4] {'band','ga'}, dimensions={0} | all-to-all | bytes 2883584 | tf_op jit(solution)/shard_map/all_to_all | solution.py:44
  238.9 0.0 copy-done
  238.9 1.4 add_convert_fusion
  (2 shorter events, 0.0 us)
Async XLA Ops:
  6.5 181.2 %all-reduce.2.cloned.1.call-start = ((), (), s32[]{:S(2)}) async-start(), calls=%async_computation.2 | async-start | bytes 3407872 | tf_op jit(solution)/shard_map/psum | solution.py:42
  57.5 0.7 copy-start.1
  57.5 0.8 copy-start.2
  198.9 40.0 %copy-start = (bf16[8,90112]{1,0:T(8,128)(2,1)S(1)}, bf16[8,90112]{1,0:T(8,128)(2,1)}, u32[]{:S(2)}) copy-start(bf16[8,90112]{1,0:T(8,128)(2,1)} %param.6) | copy-start | bytes 4325380
Sparse Core Ops, SparseCore 0:
  57.7 130.0 all-reduce.1
where the time goes:
time: 248 us; the launch traced here: 247 us
  waiting for transfers between devices  129 us (52%)
  blocking collectives  82.4 us (33%)
  matrix products  15.5 us (6%)
  between operations  13.4 us (5%)
  other arithmetic  4.41 us (2%)
    psum x1, waiting for transfers between devices, on_device(): totals = lax.psum(partial_value, ('band', 'ga'))  129 us
    all_to_all x1, blocking collectives, on_device(): lax.all_to_all(orbitals, ('band', 'ga'), split_axis=1, concat_axis=0, til...  42.4 us
    all_to_all x1, blocking collectives, on_device(): lax.all_to_all(slab_correction, ('band', 'ga'), split_axis=0, concat_axis...  40 us
    dot_general x1, matrix products, on_device(): jnp.dot(slab_orbitals, projectors, preferred_element_type=jnp.float32)  8.63 us
    dot_general x1, matrix products, expand(): jnp.einsum('bp,gp->bg', coefs, projectors, preferred_element_type=jnp.flo...  6.58 us
  transfers between devices with their start and end apart: 1, of which 1 were waited for; matrix products, arithmetic and copies ran while one was open for 0% of the time, Pallas kernels for 0%

commit v1 on v0

--- a/solution.py
+++ b/solution.py
@@ -34,12 +34,18 @@
 
 
 def on_device(orbitals, local_part, projectors, couplings, species):
+
+    def part_targets(work_x):
+        for rr in ("ga", "band"):
+            work_x = lax.psum(work_x, rr)
+        return work_x
+
     blocks = select_blocks(couplings, species)
     slab_orbitals = lax.all_to_all(
         orbitals, ("band", "ga"), split_axis=1, concat_axis=0, tiled=True
     )
     partial_value = jnp.dot(slab_orbitals, projectors, preferred_element_type=jnp.float32)
-    totals = lax.psum(partial_value, ("band", "ga"))
+    totals = part_targets(partial_value)
     slab_correction = expand(couple(totals, blocks), projectors)
     correction = lax.all_to_all(
         slab_correction, ("band", "ga"), split_axis=0, concat_axis=1, tiled=True

time: 248 us -> 249 us (level)
  local copies, waits for them, and re-layouts: 2.42 us -> 5.14 us
    psum x0 -> x1, local copies, waits for them, and re-layouts: none -> 2.73 us  [part_targets(): work_x = lax.psum(work_x, rr)]
    psum x1 -> x2, waiting for transfers between devices: 129 us -> 128 us  [part_targets(): work_x = lax.psum(work_x, rr)]
  transfers between devices with their start and end apart: 1 -> 2, of which waited for: 1 -> 2; matrix products, arithmetic and copies ran while one was open for 0% -> 0% of each run, Pallas kernels for 0% -> 0%
where the time goes in v1:
time: 249 us; the launch traced here: 248 us
  waiting for transfers between devices  128 us (51%)
  blocking collectives  82.7 us (33%)
  matrix products  14.5 us (6%)
  between operations  13.5 us (5%)
  local copies, waits for them, and re-layouts  5.14 us (2%)
  other arithmetic  4.41 us (2%)
    psum x2, waiting for transfers between devices, part_targets(): work_x = lax.psum(work_x, rr)  128 us
    all_to_all x1, blocking collectives, on_device(): lax.all_to_all(orbitals, ('band', 'ga'), split_axis=1, concat_axis=0, til...  42.4 us
    all_to_all x1, blocking collectives, on_device(): lax.all_to_all(slab_correction, ('band', 'ga'), split_axis=0, concat_axis...  40.4 us
    dot_general x1, matrix products, on_device(): jnp.dot(slab_orbitals, projectors, preferred_element_type=jnp.float32)  7.69 us
    dot_general x1, matrix products, expand(): jnp.einsum('bp,gp->bg', coefs, projectors, preferred_element_type=jnp.flo...  6.58 us
  transfers between devices with their start and end apart: 2, of which 2 were waited for; matrix products, arithmetic and copies ran while one was open for 0% of the time, Pallas kernels for 0%

profile of v1, /device:TPU:1, one launch (start us, length us, event | category | flops | bytes accessed | tf_op | source)
XLA Modules:
  0.0 248.5 jit_solution(16487304538324887462)
XLA Ops:
  6.5 0.0 all-reduce.3.cloned.1.call-start
  6.5 42.4 %all_to_all.38 = bf16[8,32,2816]{2,0,1:T(8,128)(2,1)S(1)} all-to-all(bf16[8,32,2816]{2,0,1:T(8,128)(2,1)} %bitcast.148), channel_id=1, replica_groups=mesh['band'=8,'ga'=4] {'band','ga'}, dimensions={1} | all-to-all | bytes 2883584 | tf_op jit(solution)/shard_map/all_to_all | solution.py:44
  48.9 7.7 %fusion.14 = f32[256,1664]{1,0:T(8,128)} fusion(bf16[2816,1664]{1,0:T(8,128)(2,1)} %param.7, bf16[8,32,2816]{2,0,1:T(8,128)(2,1)S(1)} %all_to_all.38), kind=kOutput, calls=%fused_computation.29 | convolution fusion | flops 2399141888 | bytes 12517376 | tf_op jit(solution)/shard_map/dot_general | solution.py:47
  56.6 0.0 all-reduce.3.cloned.1.call-update
  56.6 0.0 all-reduce.5.cloned.1.call-start
  56.7 70.2 %all-reduce.3.cloned.1.call-done = f32[256,1664]{1,0:T(8,128)} async-done(((f32[256,1664]{1,0:T(8,128)}), f32[256,1664]{1,0:T(8,128)}) %all-reduce.3.cloned.1.call-update) | async-done | bytes 1703952 | tf_op jit(solution)/shard_map/psum | solution.py:40
  126.9 2.7 %copy.6 = f32[256,1664]{0,1:T(8,128)} copy(f32[256,1664]{1,0:T(8,128)} %all-reduce.3.cloned.1.call-done) | data formatting | bytes 3407872 | tf_op jit(solution)/shard_map/psum | solution.py:40
  129.6 0.0 copy-start.1
  129.6 0.0 copy-start.2
  129.6 0.0 all-reduce.5.cloned.1.call-update
  129.6 0.7 copy-done.1
  130.4 0.1 reshape.81
  130.4 0.0 copy-done.2
  130.5 0.3 convolution_bitcast_fusion
  130.7 57.9 %all-reduce.5.cloned.1.call-done = f32[256,13,128]{0,2,1:T(8,128)} async-done(((f32[256,13,128]{0,2,1:T(8,128)}), f32[256,13,128]{0,2,1:T(8,128)}) %all-reduce.5.cloned.1.call-update) | async-done | bytes 1703952 | tf_op jit(solution)/shard_map/psum | solution.py:40
  188.7 1.6 slice_bitcast_fusion.12
  190.3 3.0 %fusion.2 = bf16[256,1664]{0,1:T(8,128)(2,1)S(1)} fusion(f32[1664]{0:T(1024)S(1)} %get-tuple-element.19, f32[256,128]{0,1:T(8,128)S(1)} %get-tuple-element.6, f32[1664]{0:T(1024)S(1)} %get-tuple-element.20, f32[256,128]{0,1:T(8,128)S(1)} %get-tuple-element.7, f32[1664]{0:T(1024)S(1)} %get-tuple-element.21, f32[256,128]{0,1:T(8,128)S(1)} %get-tuple-element.8, ...), kind=kLoop, calls=%fused_computation.5 | loop fusion | flops 11075584 | bytes 2642432 | tf_op jit(solution)/shard_map/convert_element_type | solution.py:27
  193.3 6.6 %fusion = bf16[32,8,2816]{2,1,0:T(8,128)(2,1)S(1)} fusion(bf16[256,1664]{0,1:T(8,128)(2,1)S(1)} %fusion.2, bf16[2816,1664]{1,0:T(8,128)(2,1)} %param.7), kind=kOutput, calls=%fused_computation.1 | convolution fusion | flops 2399862784 | bytes 11665408 | tf_op jit(solution)/shard_map/bp,gp->bg/dot_general | solution.py:31
  199.8 0.0 copy-start
  199.9 40.4 %all_to_all.39 = bf16[32,8,2816]{2,1,0:T(8,128)(2,1)S(1)} all-to-all(bf16[32,8,2816]{2,1,0:T(8,128)(2,1)S(1)} %fusion), channel_id=1, replica_groups=mesh['band'=8,'ga'=4] {'band','ga'}, dimensions={0} | all-to-all | bytes 2883584 | tf_op jit(solution)/shard_map/all_to_all | solution.py:50
  240.2 0.0 copy-done
  240.2 1.4 add_convert_fusion
  (2 shorter events, 0.0 us)
Async XLA Ops:
  6.5 120.3 %all-reduce.3.cloned.1.call-start = ((), (), s32[]{:S(2)}) async-start(), calls=%async_computation.2 | async-start | bytes 3407872 | tf_op jit(solution)/shard_map/psum | solution.py:40
  56.6 132.1 %all-reduce.5.cloned.1.call-start = ((), (), s32[]{:S(2)}) async-start(), calls=%async_computation.3 | async-start | bytes 3407872 | tf_op jit(solution)/shard_map/psum | solution.py:40
  129.6 0.7 copy-start.1
  129.6 0.8 copy-start.2
  199.8 40.4 %copy-start = (bf16[8,90112]{1,0:T(8,128)(2,1)S(1)}, bf16[8,90112]{1,0:T(8,128)(2,1)}, u32[]{:S(2)}) copy-start(bf16[8,90112]{1,0:T(8,128)(2,1)} %param.6) | copy-start | bytes 4325380
Sparse Core Ops, SparseCore 0:
  56.7 70.0 all-reduce.2
  130.1 58.4 all-reduce.4
